TPU v7x, 32 devices: a whole 2x2x4 slice. The times are simulated.
32 devices in a mesh: dp: 8 (over y, x, core), mp: 4 (over z).
Axes of the slice: x: 2, y: 2, z: 4, core: 2. Of those that a mesh axis runs over, the one named last changes fastest.
Arguments:
- inputs: bfloat16 [1024, 6144], P('dp'), may hold values from -6 to 6
- pre_act: bfloat16 [1024, 12288], P('dp', 'mp'), may hold values from -6 to 6
- out_grad: bfloat16 [1024, 6144], P('dp'), may hold values from -6 to 6
- w_in: bfloat16 [6144, 12288], P(None, 'mp'), may hold values from -0.109375 to 0.109375
- w_out: bfloat16 [12288, 6144], P('mp'), may hold values from -0.0546875 to 0.0546875
- master_in: float32 [6144, 12288], P('dp', 'mp'), may hold values from -0.3 to 0.3
- master_out: float32 [12288, 6144], P('mp', 'dp'), may hold values from -0.3 to 0.3
- row_in: float32 [6144], P('dp'), may hold values from 12.8 to 686.08
- col_in: float32 [12288], P('mp'), may hold values from 25 to 128
- row_out: float32 [12288], P('mp'), may hold values from 25.6 to 1372.16
- col_out: float32 [6144], P('dp'), may hold values from 51 to 256
Outputs:
- input_grad: bfloat16 [1024, 6144], P('dp', 'mp')
- new_master_in: float32 [6144, 12288], P('dp', 'mp')
- new_master_out: float32 [12288, 6144], P('mp', 'dp')
All inputs are finite; a program needn't handle non-finite values.
Results may differ from a plain program's by a relative error of at most 0.012.
Values may be sent and summed in bfloat16 or wider, within the bound.
A program may use at most 256 MiB of HBM per device.

v0:
```python
import math
import jax
import jax.numpy as jnp
from jax import lax
from jax.sharding import PartitionSpec as P

D = 6144
FF = 12288
decay_rate = 0.8
step_size = 0.05
tiny_square = 1e-30


def gelu_parts(pre):
    cumulative = 0.5 * (1.0 + jax.scipy.special.erf(pre * (1.0 / math.sqrt(2.0))))
    density = jnp.exp(-0.5 * pre * pre) * (1.0 / math.sqrt(2.0 * math.pi))
    return (pre * cumulative, cumulative + pre * density)


def contract_rows(left, right):
    return lax.dot_general(
        left, right, (((0,), (0,)), ((), ())), preferred_element_type=jnp.float32
    )


def scatter_sum(partial, axis):
    size = lax.axis_size(axis)
    me = lax.axis_index(axis)
    width = partial.shape[1] // size
    piece = lambda k: lax.dynamic_slice_in_dim(partial, k * width, width, 1)
    total = piece(me)
    for shift in range(1, size):
        moved = piece(lax.rem(me + shift, size)).astype(jnp.bfloat16)
        got = lax.ppermute(moved, axis, [(i, (i + shift) % size) for i in range(size)])
        total = total + got.astype(jnp.float32)
    return total


def body(
    inputs, pre_act, out_grad, w_in, w_out, master_in, master_out, row_in, col_in, row_out, col_out
):
    active, slope = gelu_parts(pre_act.astype(jnp.float32))
    hidden_all = lax.all_gather(active.astype(jnp.bfloat16), "dp", axis=0, tiled=True)
    out_cols = lax.all_to_all(out_grad, "dp", 1, 0, tiled=True)
    in_cols = lax.all_to_all(inputs, "dp", 1, 0, tiled=True)
    hid_grad = lax.dot_general(
        out_grad, w_out, (((1,), (1,)), ((), ())), preferred_element_type=jnp.float32
    )
    pre_grad = (hid_grad * slope).astype(jnp.bfloat16)
    pre_grad_all = lax.all_gather(pre_grad, "dp", axis=0, tiled=True)
    input_part = lax.dot_general(
        pre_grad, w_in, (((1,), (1,)), ((), ())), preferred_element_type=jnp.float32
    )
    input_grad = scatter_sum(input_part, "mp").astype(jnp.bfloat16)
    grad_out = contract_rows(hidden_all, out_cols)
    grad_in = contract_rows(in_cols, pre_grad_all)
    square_in = grad_in * grad_in + tiny_square
    square_out = grad_out * grad_out + tiny_square
    width_in, width_out, row_out_sum = lax.psum(
        (jnp.sum(square_in, axis=1), jnp.sum(square_out, axis=0), jnp.sum(row_out)), "mp"
    )
    rows_in = decay_rate * row_in + (1.0 - decay_rate) * width_in / FF
    cols_out = decay_rate * col_out + (1.0 - decay_rate) * width_out / FF
    hidden_in, hidden_out, sum_in, sum_out = lax.psum(
        (
            jnp.sum(square_in, axis=0),
            jnp.sum(square_out, axis=1),
            jnp.sum(rows_in),
            jnp.sum(width_out),
        ),
        "dp",
    )
    cols_in = decay_rate * col_in + (1.0 - decay_rate) * hidden_in / D
    rows_out = decay_rate * row_out + (1.0 - decay_rate) * hidden_out / D
    mean_in = sum_in / D
    mean_out = (decay_rate * row_out_sum + (1.0 - decay_rate) * sum_out / D) / FF
    update_in = grad_in / jnp.sqrt(rows_in[:, None] * cols_in[None, :] / mean_in)
    update_out = grad_out / jnp.sqrt(rows_out[:, None] * cols_out[None, :] / mean_out)
    new_master_in = master_in - step_size * update_in
    new_master_out = master_out - step_size * update_out
    return (input_grad, new_master_in, new_master_out)


def solution(mesh):
    in_specs = (
        P("dp", None),
        P("dp", "mp"),
        P("dp", None),
        P(None, "mp"),
        P("mp", None),
        P("dp", "mp"),
        P("mp", "dp"),
        P("dp"),
        P("mp"),
        P("mp"),
        P("dp"),
    )
    out_specs = (P("dp", "mp"), P("dp", "mp"), P("mp", "dp"))
    return jax.shard_map(body, mesh=mesh, in_specs=in_specs, out_specs=out_specs, check_vma=False)
```

profile of v0, /device:TPU:0, one launch (start us, length us, event | category | flops | bytes accessed | tf_op | source)
XLA Modules:
  0.0 242.8 jit_solution(6734764929299141886)
XLA Ops:
  7.2 0.0 copy-start.1
  7.2 0.0 all-gather.3.cloned.1.call-start
  7.2 19.2 %fusion.7 = bf16[128,3072]{1,0:T(8,128)(2,1)} fusion(bf16[128,6144]{1,0:T(8,128)(2,1)} %param.13, bf16[3072,6144]{1,0:T(8,128)(2,1)} %param.15, bf16[128,3072]{1,0:T(8,128)(2,1)} %param.12), kind=kOutput, calls=%fused_computation.12 | convolution fusion | flops 4836163584 | bytes 40894464 | tf_op jit(solution)/shard_map/dot_general | solution.py:46
  26.4 0.0 copy-start.2
  26.4 0.0 all-gather.3.cloned.1.call-update
  26.5 0.0 all-gather.5.cloned.1.call-start
  26.5 2.5 %fusion.14 = bf16[128,3072]{1,0:T(8,128)(2,1)} fusion(bf16[128,3072]{1,0:T(8,128)(2,1)} %param.12), kind=kLoop, calls=%fused_computation.24 | loop fusion | flops 2359296 | bytes 1572864 | tf_op jit(solution)/shard_map/convert_element_type | solution.py:43
  29.0 0.0 all-gather.5.cloned.1.call-update
  29.0 0.0 copy-done.1
  29.0 1.6 copy.18
  30.6 5.2 %all-to-all-start = ((bf16[128,8,768]{0,2,1:T(8,128)(2,1)}), bf16[128,8,768]{0,2,1:T(8,128)(2,1)S(1)}, u32[]{:S(2)}, u32[]{:S(2)}) async-start(bf16[128,8,768]{0,2,1:T(8,128)(2,1)} %bitcast), calls=%async_computation | async-start | bytes 3145728 | tf_op jit(solution)/shard_map/all_to_all | solution.py:45
  35.8 0.0 copy-done.2
  35.8 1.7 copy.21
  37.5 27.7 %all-to-all-done = bf16[128,8,768]{0,2,1:T(8,128)(2,1)S(1)} async-done(((bf16[128,8,768]{0,2,1:T(8,128)(2,1)}), bf16[128,8,768]{0,2,1:T(8,128)(2,1)S(1)}, u32[]{:S(2)}, u32[]{:S(2)}) %all-to-all-start) | async-done | bytes 1572896 | tf_op jit(solution)/shard_map/all_to_all | solution.py:45
  65.2 0.0 copy-start
  65.2 1.1 copy-done
  66.3 4.3 %all-to-all-start.1 = ((bf16[128,8,768]{0,2,1:T(8,128)(2,1)}), bf16[128,8,768]{0,2,1:T(8,128)(2,1)}, u32[]{:S(2)}, u32[]{:S(2)}) async-start(bf16[128,8,768]{0,2,1:T(8,128)(2,1)} %bitcast.4), calls=%async_computation.1 | async-start | bytes 3145728 | tf_op jit(solution)/shard_map/all_to_all | solution.py:44
  70.6 18.0 %fusion.16 = f32[128,6144]{1,0:T(8,128)S(1)} fusion(bf16[128,3072]{1,0:T(8,128)(2,1)} %fusion.7, bf16[6144,3072]{1,0:T(8,128)(2,1)} %param.14), kind=kOutput, calls=%fused_computation.34 | convolution fusion | flops 4831838208 | bytes 41680896 | tf_op jit(solution)/shard_map/dot_general | solution.py:51
  88.6 1.0 dynamic-slice_convert_fusion.2
  89.6 1.6 collective-permute-start
  91.2 2.5 %collective-permute-start.1 = (bf16[128,1536]{1,0:T(8,128)(2,1)}, bf16[128,1536]{1,0:T(8,128)(2,1)}, u32[]{:S(2)}, u32[]{:S(2)}) collective-permute-start(bf16[128,1536]{1,0:T(8,128)(2,1)} %get-tuple-element.27), channel_id=1, source_target_pairs={{0,2},{1,3},{2,0},{3,1},{4,6},{5,7},{6,4},{7,5},{8,10},{9,11},{10,... | collective-permute-start | bytes 1179656 | tf_op jit(solution)/shard_map/ppermute | solution.py:34
  93.7 1.4 collective-permute-start.2
  95.1 0.0 copy-start.3
  95.1 9.6 %copy.20 = f32[768,3072]{0,1:T(8,128)} copy(f32[768,3072]{1,0:T(8,128)} %param.16) | data formatting | bytes 18874368 | tf_op args[5]
  104.7 0.0 copy-done.3
  104.7 0.6 reduce_sum.68
  105.3 0.0 collective-permute-done
  105.3 14.8 %collective-permute-done.1 = bf16[128,1536]{1,0:T(8,128)(2,1)} collective-permute-done((bf16[128,1536]{1,0:T(8,128)(2,1)}, bf16[128,1536]{1,0:T(8,128)(2,1)}, u32[]{:S(2)}, u32[]{:S(2)}) %collective-permute-start.1) | collective-permute-done | bytes 393248 | tf_op jit(solution)/shard_map/ppermute | solution.py:34
  120.1 0.0 collective-permute-done.2
  120.1 2.2 add_convert_fusion
  122.3 1.7 copy.19
  124.0 0.0 all-to-all-done.1
  124.0 1.7 copy.22
  125.7 0.0 all-gather.3.cloned.1.call-done
  125.8 11.3 %fusion.5 = (f32[3072]{0:T(1024)S(1)}, f32[768]{0:T(1024)S(1)}, f32[3072,768]{1,0:T(8,128)}) fusion(bf16[1024,3072]{1,0:T(8,128)(2,1)} %all-gather.3.cloned.1.call-done, bf16[1024,768]{1,0:T(8,128)(2,1)S(1)} %bitcast.29), kind=kOutput, calls=%fused_computation.9 | convolution fusion | flops 4841271296 | bytes 17316864 | tf_op jit(solution)/shard_map/dot_general | solution.py:21
  137.0 17.9 %all-gather.5.cloned.1.call-done = bf16[1024,3072]{1,0:T(8,128)(2,1)} async-done(((bf16[128,3072]{1,0:T(8,128)(2,1)}), bf16[1024,3072]{1,0:T(8,128)(2,1)}) %all-gather.5.cloned.1.call-update) | async-done | bytes 6291472 | tf_op jit(solution)/shard_map/all_gather | solution.py:43
  155.0 0.0 copy-start.5
  155.0 0.0 copy-start.6
  155.0 0.0 copy-start.4
  155.0 11.3 %fusion.4 = (f32[3072]{0:T(1024)S(1)}, f32[768]{0:T(1024)S(1)}, f32[3072,768]{1,0:T(8,128)}) fusion(bf16[1024,3072]{1,0:T(8,128)(2,1)} %all-gather.5.cloned.1.call-done, bf16[1024,768]{1,0:T(8,128)(2,1)S(1)} %bitcast.28), kind=kOutput, calls=%fused_computation.8 | convolution fusion | flops 4841271296 | bytes 17316864 | tf_op jit(solution)/shard_map/dot_general | solution.py:21
  166.2 12.6 %all-reduce.1 = (f32[768]{0:T(1024)S(1)}, f32[768]{0:T(1024)S(1)}, f32[]{:T(128)}) all-reduce(f32[768]{0:T(1024)S(1)} %get-tuple-element.15, f32[768]{0:T(1024)S(1)} %get-tuple-element.13, f32[]{:T(128)} %reduce_sum.68), channel_id=1, replica_groups=mesh['dp'=8,'mp'=4] {'mp'}, use_global_device_ids=true, to_apply=%region_1.0 | all-reduce | flops 1537 | bytes 12296 | tf_op jit(solution)/shard_map/psum | solution.py:59
  178.8 0.0 copy-done.5
  178.8 0.0 copy-done.6
  178.8 0.7 multiply_add_fusion.3
  179.5 22.4 %all-reduce = (f32[]{:T(128)}, f32[3072]{0:T(1024)S(1)}, f32[]{:T(128)}, f32[3072]{0:T(1024)S(1)}) all-reduce(f32[]{:T(128)} %get-tuple-element.32, f32[3072]{0:T(1024)S(1)} %get-tuple-element.14, f32[]{:T(128)} %get-tuple-element.29, f32[3072]{0:T(1024)S(1)} %get-tuple-element.12), channel_id=1, replica_groups=mesh['dp'=8,'mp'=4] {'dp'}, use_global_device_ids=true, to_apply=%region_5.0 | all-reduce | flops 6146 | bytes 49168 | tf_op jit(solution)/shard_map/psum | solution.py:64
  201.9 0.0 copy-done.4
  202.6 11.2 %fusion.2 = f32[768,3072]{0,1:T(8,128)} fusion(f32[768,3072]{0,1:T(8,128)} %copy.20, f32[3072,768]{1,0:T(8,128)} %get-tuple-element.30, f32[]{:T(128)S(6)} %div.47, f32[3072]{0:T(1024)S(1)} %multiply_add_fusion.2, f32[768]{0:T(1024)S(1)} %get-tuple-element.33), kind=kLoop, calls=%fused_computation.4 | loop fusion | flops 11796480 | bytes 28326916 | tf_op jit(solution)/shard_map/sub | solution.py:79
  213.8 9.6 %copy.23 = f32[768,3072]{1,0:T(8,128)} copy(f32[768,3072]{0,1:T(8,128)} %fusion.2) | data formatting | bytes 18874368
  224.7 11.3 %multiply_subtract_fusion = f32[3072,768]{1,0:T(8,128)} fusion(f32[3072,768]{1,0:T(8,128)} %param.17, f32[3072,768]{1,0:T(8,128)} %get-tuple-element.31, f32[]{:T(128)S(6)} %div.54, f32[768]{0:T(1024)S(1)} %get-tuple-element.28, f32[3072]{0:T(1024)S(1)} %multiply_add_fusion.1), kind=kLoop, calls=%fused_computation.5 | loop fusion | flops 11796480 | bytes 28326916 | tf_op jit(solution)/shard_map/sub | solution.py:80
  (2 shorter events, 0.0 us)
Async XLA Ops:
  7.2 21.9 %copy-start.1 = (bf16[128,6144]{1,0:T(8,128)(2,1)S(1)}, bf16[128,6144]{1,0:T(8,128)(2,1)}, u32[]{:S(2)}) copy-start(bf16[128,6144]{1,0:T(8,128)(2,1)} %param.11) | copy-start | bytes 4718596
  7.2 118.6 %all-gather.3.cloned.1.call-start = ((), (), s32[]{:S(2)}) async-start(), calls=%async_computation.2 | async-start | bytes 7077888 | tf_op jit(solution)/shard_map/all_gather | solution.py:50
  26.4 9.4 %copy-start.2 = (bf16[128,6144]{1,0:T(8,128)(2,1)S(1)}, bf16[128,6144]{1,0:T(8,128)(2,1)}, u32[]{:S(2)}) copy-start(bf16[128,6144]{1,0:T(8,128)(2,1)} %param.13) | copy-start | bytes 4718596
  26.5 128.5 %all-gather.5.cloned.1.call-start = ((), (), s32[]{:S(2)}) async-start(), calls=%async_computation.3 | async-start | bytes 7077888 | tf_op jit(solution)/shard_map/all_gather | solution.py:43
  30.6 34.6 %all-to-all-start = ((bf16[128,8,768]{0,2,1:T(8,128)(2,1)}), bf16[128,8,768]{0,2,1:T(8,128)(2,1)S(1)}, u32[]{:S(2)}, u32[]{:S(2)}) async-start(bf16[128,8,768]{0,2,1:T(8,128)(2,1)} %bitcast), calls=%async_computation | async-start | bytes 3145728 | tf_op jit(solution)/shard_map/all_to_all | solution.py:45
  65.2 1.1 copy-start
  66.3 57.7 %all-to-all-start.1 = ((bf16[128,8,768]{0,2,1:T(8,128)(2,1)}), bf16[128,8,768]{0,2,1:T(8,128)(2,1)}, u32[]{:S(2)}, u32[]{:S(2)}) async-start(bf16[128,8,768]{0,2,1:T(8,128)(2,1)} %bitcast.4), calls=%async_computation.1 | async-start | bytes 3145728 | tf_op jit(solution)/shard_map/all_to_all | solution.py:44
  89.6 15.7 %collective-permute-start = (bf16[128,1536]{1,0:T(8,128)(2,1)}, bf16[128,1536]{1,0:T(8,128)(2,1)}, u32[]{:S(2)}, u32[]{:S(2)}) collective-permute-start(bf16[128,1536]{1,0:T(8,128)(2,1)} %get-tuple-element.25), channel_id=1, source_target_pairs={{0,1},{1,2},{2,3},{3,0},{4,5},{5,6},{6,7},{7,4},{8,9},{9,10},{10,1... | collective-permute-start | bytes 1179656 | tf_op jit(solution)/shard_map/ppermute | solution.py:34
  91.2 28.9 %collective-permute-start.1 = (bf16[128,1536]{1,0:T(8,128)(2,1)}, bf16[128,1536]{1,0:T(8,128)(2,1)}, u32[]{:S(2)}, u32[]{:S(2)}) collective-permute-start(bf16[128,1536]{1,0:T(8,128)(2,1)} %get-tuple-element.27), channel_id=1, source_target_pairs={{0,2},{1,3},{2,0},{3,1},{4,6},{5,7},{6,4},{7,5},{8,10},{9,11},{10,... | collective-permute-start | bytes 1179656 | tf_op jit(solution)/shard_map/ppermute | solution.py:34
  93.7 26.4 %collective-permute-start.2 = (bf16[128,1536]{1,0:T(8,128)(2,1)S(1)}, bf16[128,1536]{1,0:T(8,128)(2,1)}, u32[]{:S(2)}, u32[]{:S(2)}) collective-permute-start(bf16[128,1536]{1,0:T(8,128)(2,1)S(1)} %get-tuple-element.26), channel_id=1, source_target_pairs={{0,3},{1,0},{2,1},{3,2},{4,7},{5,4},{6,5},{7,6},{8,11},{9,8},{10,9... | collective-permute-start | bytes 1179656 | tf_op jit(solution)/shard_map/ppermute | solution.py:34
  95.1 9.6 %copy-start.3 = (f32[3072]{0:T(1024)S(1)}, f32[3072]{0:T(1024)}, u32[]{:S(2)}) copy-start(f32[3072]{0:T(1024)} %param.20) | copy-start | bytes 36868
  155.0 23.9 %copy-start.5 = (f32[768]{0:T(1024)S(1)}, f32[768]{0:T(1024)}, u32[]{:S(2)}) copy-start(f32[768]{0:T(1024)} %param.21) | copy-start | bytes 9220
  155.0 23.9 %copy-start.6 = (f32[768]{0:T(1024)S(1)}, f32[768]{0:T(1024)}, u32[]{:S(2)}) copy-start(f32[768]{0:T(1024)} %param.18) | copy-start | bytes 9220
  155.0 47.0 %copy-start.4 = (f32[3072]{0:T(1024)S(1)}, f32[3072]{0:T(1024)}, u32[]{:S(2)}) copy-start(f32[3072]{0:T(1024)} %param.19) | copy-start | bytes 36868
Sparse Core Ops, SparseCore 0:
  26.6 79.3 all-gather.2
  107.8 47.0 all-gather.4
where the time goes:
time: 243 us
  waiting for transfers between devices  60.5 us (25%)
  matrix products  59.7 us (25%)
  blocking collectives  35 us (14%)
  other arithmetic  28.4 us (12%)
  local copies, waits for them, and re-layouts  28 us (12%)
  between operations  16.1 us (7%)
  starting transfers between devices  15 us (6%)
    all_to_all x1, waiting for transfers between devices, body(): in_cols = lax.all_to_all(inputs, 'dp', 1, 0, tiled=True)  27.7 us
    unnamed x18, local copies, waits for them, and re-layouts  23.6 us
    dot_general x2, matrix products, contract_rows(): lax.dot_general(left, right, (((0,), (0,)), ((), ())), preferred_element_...  22.6 us
    psum x1, blocking collectives, body(): lax.psum((jnp.sum(square_in, axis=0), jnp.sum(square_out, axis=1), jnp.su...  22.4 us
    dot_general x1, matrix products, body(): lax.dot_general(out_grad, w_out, (((1,), (1,)), ((), ())), preferred_elem...  19.2 us
    dot_general x1, matrix products, body(): lax.dot_general(pre_grad, w_in, (((1,), (1,)), ((), ())), preferred_eleme...  18 us
    all_gather x1, waiting for transfers between devices, body(): lax.all_gather(active.astype(jnp.bfloat16), 'dp', axis=0, tiled=True)  17.9 us
    ppermute x3, waiting for transfers between devices, scatter_sum(): lax.ppermute(moved, axis, [(i, (i + shift) % size) for i in range(size)])  14.8 us
  transfers between devices with their start and end apart: 7, of which 3 were waited for; matrix products, arithmetic and copies ran while one was open for 21% of the time, Pallas kernels for 0%

commit v1 on v0

--- a/solution.py
+++ b/solution.py
@@ -42,7 +42,10 @@
     active, slope = gelu_parts(pre_act.astype(jnp.float32))
     hidden_all = lax.all_gather(active.astype(jnp.bfloat16), "dp", axis=0, tiled=True)
     out_cols = lax.all_to_all(out_grad, "dp", 1, 0, tiled=True)
-    in_cols = lax.all_to_all(inputs, "dp", 1, 0, tiled=True)
+    in_cols = jnp.concatenate(
+        lax.all_to_all(jnp.stack(jnp.split(inputs, lax.axis_size("dp"), axis=1)), "dp", 0, 0),
+        axis=0,
+    )
     hid_grad = lax.dot_general(
         out_grad, w_out, (((1,), (1,)), ((), ())), preferred_element_type=jnp.float32
     )

time: 243 us -> 230 us (0.947)
  local copies, waits for them, and re-layouts: 28 us -> 14.2 us
  waiting for transfers between devices: 60.5 us -> 68.7 us
  other arithmetic: 28.4 us -> 21.8 us
    all_to_all x1, waiting for transfers between devices: 27.7 us -> 0.01 us  [body(): lax.all_to_all(jnp.stack(jnp.split(inputs, lax.axis_size('dp'), axis=1)),...]
    all_to_all x1, waiting for transfers between devices: 0.01 us -> 23.8 us  [body(): out_cols = lax.all_to_all(out_grad, 'dp', 1, 0, tiled=True)]
    unnamed x18 -> x36, local copies, waits for them, and re-layouts: 23.6 us -> 10.8 us
    ppermute x3, waiting for transfers between devices: 14.8 us -> 24.4 us  [scatter_sum(): lax.ppermute(moved, axis, [(i, (i + shift) % size) for i in range(size)])]
    sub x1, other arithmetic: 11.2 us -> 5.06 us  [body(): new_master_in = master_in - step_size * update_in]
    all_gather x1, waiting for transfers between devices: 17.9 us -> 20.4 us  [body(): lax.all_gather(active.astype(jnp.bfloat16), 'dp', axis=0, tiled=True)]
  transfers between devices with their start and end apart: 7 -> 7, of which waited for: 3 -> 4; matrix products, arithmetic and copies ran while one was open for 21% -> 18% of each run, Pallas kernels for 0% -> 0%
where the time goes in v1:
time: 230 us
  waiting for transfers between devices  68.7 us (30%)
  matrix products  58.9 us (26%)
  blocking collectives  35 us (15%)
  other arithmetic  21.8 us (9%)
  between operations  16.1 us (7%)
  starting transfers between devices  15.1 us (7%)
  local copies, waits for them, and re-layouts  14.2 us (6%)
    ppermute x3, waiting for transfers between devices, scatter_sum(): lax.ppermute(moved, axis, [(i, (i + shift) % size) for i in range(size)])  24.4 us
    all_to_all x1, waiting for transfers between devices, body(): out_cols = lax.all_to_all(out_grad, 'dp', 1, 0, tiled=True)  23.8 us
    psum x1, blocking collectives, body(): lax.psum((jnp.sum(square_in, axis=0), jnp.sum(square_out, axis=1), jnp.su...  22.4 us
    dot_general x2, matrix products, contract_rows(): lax.dot_general(left, right, (((0,), (0,)), ((), ())), preferred_element_...  21.8 us
    all_gather x1, waiting for transfers between devices, body(): lax.all_gather(active.astype(jnp.bfloat16), 'dp', axis=0, tiled=True)  20.4 us
    dot_general x1, matrix products, body(): lax.dot_general(out_grad, w_out, (((1,), (1,)), ((), ())), preferred_elem...  19.1 us
    dot_general x1, matrix products, body(): lax.dot_general(pre_grad, w_in, (((1,), (1,)), ((), ())), preferred_eleme...  17.9 us
    psum x1, blocking collectives, body(): lax.psum((jnp.sum(square_in, axis=1), jnp.sum(square_out, axis=0), jnp.su...  12.5 us
  transfers between devices with their start and end apart: 7, of which 4 were waited for; matrix products, arithmetic and copies ran while one was open for 18% of the time, Pallas kernels for 0%

profile of v1, /device:TPU:0, one launch (start us, length us, event | category | flops | bytes accessed | tf_op | source)
XLA Modules:
  0.0 229.9 jit_solution(6014334119231437913)
XLA Ops:
  7.2 0.0 copy-start.3
  7.2 0.0 all-gather.3.cloned.1.call-start
  7.2 19.1 %fusion.4 = bf16[128,3072]{1,0:T(8,128)(2,1)} fusion(bf16[128,6144]{1,0:T(8,128)(2,1)} %param.13, bf16[3072,6144]{1,0:T(8,128)(2,1)} %param.15, bf16[128,3072]{1,0:T(8,128)(2,1)} %param.12), kind=kOutput, calls=%fused_computation.9 | convolution fusion | flops 4836163584 | bytes 40894464 | tf_op jit(solution)/shard_map/dot_general | solution.py:49
  26.4 0.0 copy-start.1
  26.4 0.0 all-gather.3.cloned.1.call-update
  26.4 0.0 all-gather.5.cloned.1.call-start
  26.4 0.0 copy-done.3
  26.4 1.2 fusion.11
  27.7 0.0 all-gather.5.cloned.1.call-update
  27.7 0.2 copy-done.1
  27.9 1.6 copy.14
  29.4 0.0 copy-start.2
  29.4 5.3 %all-to-all-start.1 = ((bf16[128,8,768]{0,2,1:T(8,128)(2,1)}), bf16[128,8,768]{0,2,1:T(8,128)(2,1)S(1)}, u32[]{:S(2)}, u32[]{:S(2)}) async-start(bf16[128,8,768]{0,2,1:T(8,128)(2,1)} %bitcast.9), calls=%async_computation.1 | async-start | bytes 3145728 | tf_op jit(solution)/shard_map/all_to_all | solution.py:44
  34.8 0.0 copy-done.2
  34.8 0.7 bitcast_dynamic-update-slice_fusion.7
  35.5 0.7 bitcast_dynamic-update-slice_fusion.6
  36.1 0.7 bitcast_dynamic-update-slice_fusion.5
  36.8 0.7 bitcast_dynamic-update-slice_fusion.4
  37.5 0.7 bitcast_dynamic-update-slice_fusion.3
  38.2 0.7 bitcast_dynamic-update-slice_fusion.2
  38.9 0.7 bitcast_dynamic-update-slice_fusion.1
  39.6 0.7 bitcast_dynamic-update-slice_fusion
  40.3 23.8 %all-to-all-done.1 = bf16[128,8,768]{0,2,1:T(8,128)(2,1)S(1)} async-done(((bf16[128,8,768]{0,2,1:T(8,128)(2,1)}), bf16[128,8,768]{0,2,1:T(8,128)(2,1)S(1)}, u32[]{:S(2)}, u32[]{:S(2)}) %all-to-all-start.1) | async-done | bytes 1572896 | tf_op jit(solution)/shard_map/all_to_all | solution.py:44
  64.1 0.0 copy-start
  64.1 1.1 copy-done
  65.3 4.3 %all-to-all-start = ((bf16[8,128,768]{2,1,0:T(8,128)(2,1)}), bf16[8,128,768]{2,1,0:T(8,128)(2,1)}, u32[]{:S(2)}, u32[]{:S(2)}) async-start(bf16[8,128,768]{2,1,0:T(8,128)(2,1)} %bitcast_dynamic-update-slice_fusion), calls=%async_computation | async-start | bytes 3145728 | tf_op jit(solution)/shard_map/all_to_all | solution.py:46
  69.6 17.9 %fusion.13 = f32[128,6144]{1,0:T(8,128)S(1)} fusion(bf16[128,3072]{1,0:T(8,128)(2,1)} %fusion.4, bf16[6144,3072]{1,0:T(8,128)(2,1)} %param.14), kind=kOutput, calls=%fused_computation.39 | convolution fusion | flops 4831838208 | bytes 41680896 | tf_op jit(solution)/shard_map/dot_general | solution.py:54
  87.5 0.0 copy-start.4
  87.6 1.0 dynamic-slice_convert_fusion.2
  88.6 1.6 collective-permute-start
  90.2 2.5 %collective-permute-start.1 = (bf16[128,1536]{1,0:T(8,128)(2,1)}, bf16[128,1536]{1,0:T(8,128)(2,1)}, u32[]{:S(2)}, u32[]{:S(2)}) collective-permute-start(bf16[128,1536]{1,0:T(8,128)(2,1)} %get-tuple-element.18), channel_id=1, source_target_pairs={{0,2},{1,3},{2,0},{3,1},{4,6},{5,7},{6,4},{7,5},{8,10},{9,11},{10,... | collective-permute-start | bytes 1179656 | tf_op jit(solution)/shard_map/ppermute | solution.py:34
  92.7 1.4 collective-permute-start.2
  94.0 0.0 copy-done.4
  94.0 0.6 reduce_sum.68
  94.7 8.2 %collective-permute-done = bf16[128,1536]{1,0:T(8,128)(2,1)} collective-permute-done((bf16[128,1536]{1,0:T(8,128)(2,1)}, bf16[128,1536]{1,0:T(8,128)(2,1)}, u32[]{:S(2)}, u32[]{:S(2)}) %collective-permute-start) | collective-permute-done | bytes 393248 | tf_op jit(solution)/shard_map/ppermute | solution.py:34
  102.8 16.3 %collective-permute-done.1 = bf16[128,1536]{1,0:T(8,128)(2,1)} collective-permute-done((bf16[128,1536]{1,0:T(8,128)(2,1)}, bf16[128,1536]{1,0:T(8,128)(2,1)}, u32[]{:S(2)}, u32[]{:S(2)}) %collective-permute-start.1) | collective-permute-done | bytes 393248 | tf_op jit(solution)/shard_map/ppermute | solution.py:34
  119.1 0.0 collective-permute-done.2
  119.1 2.2 add_convert_fusion
  121.3 1.7 copy.15
  123.0 0.0 all-to-all-done
  123.0 0.0 all-gather.3.cloned.1.call-done
  123.0 10.5 %fusion = (f32[3072]{0:T(1024)S(1)}, f32[768]{0:T(1024)S(1)}, f32[768,3072]{1,0:T(8,128)}) fusion(bf16[1024,768]{1,0:T(8,128)(2,1)} %bitcast.8, bf16[1024,3072]{1,0:T(8,128)(2,1)} %all-gather.3.cloned.1.call-done), kind=kOutput, calls=%fused_computation.4 | convolution fusion | flops 4841271296 | bytes 17316864 | tf_op jit(solution)/shard_map/dot_general | solution.py:21
  133.5 20.4 %all-gather.5.cloned.1.call-done = bf16[1024,3072]{1,0:T(8,128)(2,1)} async-done(((bf16[128,3072]{1,0:T(8,128)(2,1)}), bf16[1024,3072]{1,0:T(8,128)(2,1)}) %all-gather.5.cloned.1.call-update) | async-done | bytes 6291472 | tf_op jit(solution)/shard_map/all_gather | solution.py:43
  153.9 11.3 %fusion.3 = (f32[3072]{0:T(1024)S(1)}, f32[768]{0:T(1024)S(1)}, f32[3072,768]{1,0:T(8,128)}) fusion(bf16[1024,3072]{1,0:T(8,128)(2,1)} %all-gather.5.cloned.1.call-done, bf16[1024,768]{1,0:T(8,128)(2,1)S(1)} %bitcast.33), kind=kOutput, calls=%fused_computation.7 | convolution fusion | flops 4841271296 | bytes 17316864 | tf_op jit(solution)/shard_map/dot_general | solution.py:21
  165.2 12.5 %all-reduce.1 = (f32[768]{0:T(1024)S(1)}, f32[768]{0:T(1024)S(1)}, f32[]{:T(128)}) all-reduce(f32[768]{0:T(1024)S(1)} %get-tuple-element.6, f32[768]{0:T(1024)S(1)} %get-tuple-element.4, f32[]{:T(128)} %reduce_sum.68), channel_id=1, replica_groups=mesh['dp'=8,'mp'=4] {'mp'}, use_global_device_ids=true, to_apply=%region_1.0 | all-reduce | flops 1537 | bytes 12296 | tf_op jit(solution)/shard_map/psum | solution.py:62
  177.8 0.0 copy-done.6
  177.8 0.0 copy-done.7
  177.8 0.6 multiply_add_fusion.4
  178.4 22.4 %all-reduce = (f32[]{:T(128)}, f32[3072]{0:T(1024)S(1)}, f32[]{:T(128)}, f32[3072]{0:T(1024)S(1)}) all-reduce(f32[]{:T(128)} %get-tuple-element.23, f32[3072]{0:T(1024)S(1)} %get-tuple-element.5, f32[]{:T(128)} %get-tuple-element.20, f32[3072]{0:T(1024)S(1)} %get-tuple-element.3), channel_id=1, replica_groups=mesh['dp'=8,'mp'=4] {'dp'}, use_global_device_ids=true, to_apply=%region_5.0 | all-reduce | flops 6146 | bytes 49168 | tf_op jit(solution)/shard_map/psum | solution.py:67
  202.1 0.0 copy-done.5
  202.8 0.0 slice-start
  202.8 0.0 slice-start.3
  202.8 0.0 slice-start.1
  202.8 0.0 slice-start.2
  202.8 0.0 slice-start.4
  202.8 0.0 slice-start.5
  202.8 12.1 %multiply_subtract_fusion = f32[3072,768]{1,0:T(8,128)} fusion(f32[3072,768]{1,0:T(8,128)} %param.17, f32[3072,768]{1,0:T(8,128)} %get-tuple-element.22, f32[]{:T(128)S(6)} %div.54, f32[768]{0:T(1024)S(1)} %get-tuple-element.19, f32[3072]{0:T(1024)S(1)} %multiply_add_fusion.2), kind=kLoop, calls=%fused_computation | loop fusion | flops 11796480 | bytes 28326916 | tf_op jit(solution)/shard_map/sub | solution.py:83
  214.9 0.0 slice-done
  214.9 0.0 slice-done.3
  214.9 1.3 slice-done.1
  216.3 0.2 slice-done.2
  216.5 1.3 slice-done.4
  217.8 0.2 slice-done.5
  218.0 5.1 %multiply_subtract_fusion.1 = f32[768,3072]{1,0:T(8,128)} fusion(f32[768,3072]{1,0:T(8,128)S(1)} %bitcast.29, f32[768,3072]{1,0:T(8,128)S(1)} %bitcast.31, f32[]{:T(128)S(6)} %div.47, f32[3072]{0:T(1024)S(1)} %multiply_add_fusion.3, f32[768]{0:T(1024)S(1)} %get-tuple-element.24), kind=kLoop, calls=%fused_computation.2 | loop fusion | flops 11796480 | bytes 28326916 | tf_op jit(solution)/shard_map/sub | solution.py:82
  (7 shorter events, 0.0 us)
Async XLA Ops:
  7.2 19.3 %copy-start.3 = (bf16[128,3072]{1,0:T(8,128)(2,1)S(1)}, bf16[128,3072]{1,0:T(8,128)(2,1)}, u32[]{:S(2)}) copy-start(bf16[128,3072]{1,0:T(8,128)(2,1)} %param.12) | copy-start | bytes 2359300
  7.2 115.8 %all-gather.3.cloned.1.call-start = ((), (), s32[]{:S(2)}) async-start(), calls=%async_computation.2 | async-start | bytes 7077888 | tf_op jit(solution)/shard_map/all_gather | solution.py:53
  26.4 1.5 copy-start.1
  26.4 127.5 %all-gather.5.cloned.1.call-start = ((), (), s32[]{:S(2)}) async-start(), calls=%async_computation.3 | async-start | bytes 7077888 | tf_op jit(solution)/shard_map/all_gather | solution.py:43
  29.4 5.3 %copy-start.2 = (bf16[128,6144]{1,0:T(8,128)(2,1)S(1)}, bf16[128,6144]{1,0:T(8,128)(2,1)}, u32[]{:S(2)}) copy-start(bf16[128,6144]{1,0:T(8,128)(2,1)} %param.11) | copy-start | bytes 4718596
  29.4 34.7 %all-to-all-start.1 = ((bf16[128,8,768]{0,2,1:T(8,128)(2,1)}), bf16[128,8,768]{0,2,1:T(8,128)(2,1)S(1)}, u32[]{:S(2)}, u32[]{:S(2)}) async-start(bf16[128,8,768]{0,2,1:T(8,128)(2,1)} %bitcast.9), calls=%async_computation.1 | async-start | bytes 3145728 | tf_op jit(solution)/shard_map/all_to_all | solution.py:44
  64.1 1.1 copy-start
  65.3 57.7 %all-to-all-start = ((bf16[8,128,768]{2,1,0:T(8,128)(2,1)}), bf16[8,128,768]{2,1,0:T(8,128)(2,1)}, u32[]{:S(2)}, u32[]{:S(2)}) async-start(bf16[8,128,768]{2,1,0:T(8,128)(2,1)} %bitcast_dynamic-update-slice_fusion), calls=%async_computation | async-start | bytes 3145728 | tf_op jit(solution)/shard_map/all_to_all | solution.py:46
  87.5 6.5 %copy-start.4 = (f32[3072]{0:T(1024)S(1)}, f32[3072]{0:T(1024)}, u32[]{:S(2)}) copy-start(f32[3072]{0:T(1024)} %param.20) | copy-start | bytes 36868
  88.6 14.2 %collective-permute-start = (bf16[128,1536]{1,0:T(8,128)(2,1)}, bf16[128,1536]{1,0:T(8,128)(2,1)}, u32[]{:S(2)}, u32[]{:S(2)}) collective-permute-start(bf16[128,1536]{1,0:T(8,128)(2,1)} %get-tuple-element.16), channel_id=1, source_target_pairs={{0,1},{1,2},{2,3},{3,0},{4,5},{5,6},{6,7},{7,4},{8,9},{9,10},{10,1... | collective-permute-start | bytes 1179656 | tf_op jit(solution)/shard_map/ppermute | solution.py:34
  90.2 28.9 %collective-permute-start.1 = (bf16[128,1536]{1,0:T(8,128)(2,1)}, bf16[128,1536]{1,0:T(8,128)(2,1)}, u32[]{:S(2)}, u32[]{:S(2)}) collective-permute-start(bf16[128,1536]{1,0:T(8,128)(2,1)} %get-tuple-element.18), channel_id=1, source_target_pairs={{0,2},{1,3},{2,0},{3,1},{4,6},{5,7},{6,4},{7,5},{8,10},{9,11},{10,... | collective-permute-start | bytes 1179656 | tf_op jit(solution)/shard_map/ppermute | solution.py:34
  92.7 26.4 %collective-permute-start.2 = (bf16[128,1536]{1,0:T(8,128)(2,1)S(1)}, bf16[128,1536]{1,0:T(8,128)(2,1)}, u32[]{:S(2)}, u32[]{:S(2)}) collective-permute-start(bf16[128,1536]{1,0:T(8,128)(2,1)S(1)} %get-tuple-element.17), channel_id=1, source_target_pairs={{0,3},{1,0},{2,1},{3,2},{4,7},{5,4},{6,5},{7,6},{8,11},{9,8},{10,9... | collective-permute-start | bytes 1179656 | tf_op jit(solution)/shard_map/ppermute | solution.py:34
  153.9 23.9 %copy-start.6 = (f32[768]{0:T(1024)S(1)}, f32[768]{0:T(1024)}, u32[]{:S(2)}) copy-start(f32[768]{0:T(1024)} %param.21) | copy-start | bytes 9220
  153.9 23.9 %copy-start.7 = (f32[768]{0:T(1024)S(1)}, f32[768]{0:T(1024)}, u32[]{:S(2)}) copy-start(f32[768]{0:T(1024)} %param.18) | copy-start | bytes 9220
  153.9 48.2 %copy-start.5 = (f32[3072]{0:T(1024)S(1)}, f32[3072]{0:T(1024)}, u32[]{:S(2)}) copy-start(f32[3072]{0:T(1024)} %param.19) | copy-start | bytes 36868
  202.8 12.2 %slice-start = ((s8[9437184]{0:T(1024)(128)(4,1)}), s8[4194304]{0:T(1024)(128)(4,1)S(1)}, s32[]{:S(2)}) async-start(s8[9437184]{0:T(1024)(128)(4,1)} %bitcast.28), calls=%async_computation.4 | async-start | bytes 8388608
  202.8 12.2 %slice-start.3 = ((s8[9437184]{0:T(1024)(128)(4,1)}), s8[4194304]{0:T(1024)(128)(4,1)S(1)}, s32[]{:S(2)}) async-start(s8[9437184]{0:T(1024)(128)(4,1)} %bitcast.30), calls=%async_computation.7 | async-start | bytes 8388608
  202.8 13.5 %slice-start.1 = ((s8[9437184]{0:T(1024)(128)(4,1)}), s8[4194304]{0:T(1024)(128)(4,1)S(1)}, s32[]{:S(2)}) async-start(s8[9437184]{0:T(1024)(128)(4,1)} %bitcast.28), calls=%async_computation.5 | async-start | bytes 8388608
  202.8 13.7 %slice-start.2 = ((s8[9437184]{0:T(1024)(128)(4,1)}), s8[1048576]{0:T(1024)(128)(4,1)S(1)}, s32[]{:S(2)}) async-start(s8[9437184]{0:T(1024)(128)(4,1)} %bitcast.28), calls=%async_computation.6 | async-start | bytes 2097152
  202.8 15.0 %slice-start.4 = ((s8[9437184]{0:T(1024)(128)(4,1)}), s8[4194304]{0:T(1024)(128)(4,1)S(1)}, s32[]{:S(2)}) async-start(s8[9437184]{0:T(1024)(128)(4,1)} %bitcast.30), calls=%async_computation.8 | async-start | bytes 8388608
  202.8 15.2 %slice-start.5 = ((s8[9437184]{0:T(1024)(128)(4,1)}), s8[1048576]{0:T(1024)(128)(4,1)S(1)}, s32[]{:S(2)}) async-start(s8[9437184]{0:T(1024)(128)(4,1)} %bitcast.30), calls=%async_computation.9 | async-start | bytes 2097152
Sparse Core Ops, SparseCore 0:
  26.5 78.3 all-gather.2
  106.8 47.0 all-gather.4
